TPU v7x, 32 devices: a whole 2x2x4 slice. The times are simulated.
32 devices in a mesh: gx: 4 (over y, core), gy: 4 (over z), gz: 2 (over x).
Axes of the slice: x: 2, y: 2, z: 4, core: 2. Of those that a mesh axis runs over, the one named last changes fastest.
Arguments:
- face_blocks: float32 [4, 4, 2, 6, 16384], P('gx', 'gy', 'gz'), may hold values from -6 to 6
- owner_rank: int32 [4, 4, 2, 6, 1], P('gx', 'gy', 'gz'), may hold values from 0 to 3; in each aligned block of 6 rows (0 to 5, 6 to 11, ..., all dimensions but the last counted through in order) at most 2 rows name the same one
- owner_tile: int32 [4, 4, 2, 6], P('gx', 'gy', 'gz'), may hold values from 0 to 31
- live_count: int32 [4, 4, 2], P('gx', 'gy', 'gz'), may hold values from 1 to 6, as said below
- right_side: float32 [64, 256, 256], P('gx', 'gy', 'gz'), may hold values from -8 to 8
- diagonal: float32 [64, 256, 256], P('gx', 'gy', 'gz'), may hold values from 0.05 to 1
Outputs:
- solution_field: float32 [64, 256, 256], P('gx', 'gy', 'gz')
- residual: float32 [64, 256, 256], P('gx', 'gy', 'gz')
Inputs may be any that keep to these rules, and one draw needn't show every extreme that they name: `owner_rank`: on one device no owner is named by more than 2 of the 6 slots, live or not; some owner is named exactly 2 times on some devices. `live_count`: some device has all 6 slots live in every draw.
All inputs are finite; a program needn't handle non-finite values.
Results may differ from a plain program's by a relative error of at most 0.00012.
Values sent between devices are 32-bit elements; how exact they have to be, the bound alone decides.
No kernel may reach another device: no remote copies, remote signals or barrier semaphores. Data moves between devices by JAX's collectives and lax.ppermute only.
A program may use at most 64 MiB of HBM per device.

v0:
```python
import jax
import jax.numpy as jnp
from jax import lax
from jax.sharding import PartitionSpec as P

BLK = 128
CAP = 2
ITERS = 2


def padded_2(cells, sides, width):
    for axis, dim in sides:
        count = lax.axis_size(axis)
        ends = count - 1
        head = lax.slice_in_dim(cells, 0, width, axis=dim)
        tail = lax.slice_in_dim(cells, cells.shape[dim] - width, cells.shape[dim], axis=dim)
        cells = jnp.concatenate(
            [
                lax.ppermute(tail, axis, [(i, (i + 1) % count) for i in range(ends)]),
                cells,
                lax.ppermute(head, axis, [((i + 1) % count, i) for i in range(ends)]),
            ],
            axis=dim,
        )
    return cells


def restrict(values):
    half = BLK // 2
    shaped = values.reshape(values.shape[:-1] + (half, 2, half, 2))
    summed = 0.25 * jnp.sum(shaped, axis=(-3, -1))
    return summed.reshape(values.shape[:-1] + (half * half,))


def operate(field, diagonal):
    padded = padded_2(field, (("gx", 0), ("gy", 1), ("gz", 2)), 1)
    beside = padded[2:, 1:-1, 1:-1] + padded[:-2, 1:-1, 1:-1]
    beside = beside + padded[1:-1, 2:, 1:-1] + padded[1:-1, :-2, 1:-1]
    beside = beside + padded[1:-1, 1:-1, 2:] + padded[1:-1, 1:-1, :-2]
    return (6.0 + diagonal) * field - beside


def paired(residual, image):
    return lax.psum((jnp.sum(residual * residual), jnp.sum(residual * image)), ("gx", "gy", "gz"))


def per_device(face_blocks, owner_rank, owner_tile, live_count, right_side, diagonal):
    block_count = face_blocks.shape[3]
    block_width = face_blocks.shape[4]
    block_rows = face_blocks.reshape(block_count, block_width)
    group_size = lax.axis_size("gx")
    order = jnp.arange(block_count, dtype=jnp.int32)
    living = order < live_count.reshape(())
    target = owner_rank.reshape(block_count)
    before_mask = (
        (target[:, None] == target[None, :]) & (order[None, :] < order[:, None]) & living[None, :]
    )
    position = jnp.sum(before_mask.astype(jnp.int32), axis=1)
    destination_slot = target * CAP + position
    slot_range = jnp.arange(group_size * CAP, dtype=jnp.int32)
    packing = ((destination_slot[None, :] == slot_range[:, None]) & living[None, :]).astype(
        jnp.float32
    )
    tile_labels = (owner_tile.reshape(block_count) + 1).astype(jnp.float32)
    labels = jnp.dot(packing, tile_labels, precision=lax.Precision.HIGHEST).reshape(group_size, CAP)
    packed = jnp.dot(packing, block_rows, precision=lax.Precision.HIGHEST)
    received, received_tags = (
        lax.all_to_all(
            packed.reshape(group_size, CAP, -1), "gx", split_axis=0, concat_axis=0, tiled=True
        ),
        lax.all_to_all(labels, "gx", split_axis=0, concat_axis=0, tiled=True),
    )
    layers = right_side.shape[0]
    incoming = received.reshape(group_size * CAP, -1)
    tag_flat = received_tags.reshape(group_size * CAP)
    tile_range = (jnp.arange(2 * layers, dtype=jnp.int32) + 1).astype(jnp.float32)
    placing = (tag_flat[None, :] == tile_range[:, None]).astype(jnp.float32)
    tile_sums = jnp.dot(placing, incoming, precision=lax.Precision.HIGHEST)
    tile_sums = restrict(tile_sums)
    half = BLK // 2
    source = jnp.transpose(tile_sums.reshape(layers, 2, half, half), (0, 2, 1, 3)).reshape(
        layers, half, 2 * half
    )
    load = right_side + source
    solution_field = jnp.zeros_like(load)
    residual = load
    image = operate(residual, diagonal)
    norm_now, product = paired(residual, image)
    alpha = norm_now / product
    direction, along = (residual, image)
    for iteration in range(ITERS):
        solution_field = solution_field + alpha * direction
        residual = residual - alpha * along
        if iteration + 1 < ITERS:
            image = operate(residual, diagonal)
            norm_next, product = paired(residual, image)
            ratio = norm_next / norm_now
            alpha = norm_next / (product - ratio * norm_next / alpha)
            direction = residual + ratio * direction
            along = image + ratio * along
            norm_now = norm_next
    return (solution_field, residual)


def solution(mesh):
    return jax.shard_map(
        per_device,
        mesh=mesh,
        in_specs=(
            P("gx", "gy", "gz", None, None),
            P("gx", "gy", "gz", None, None),
            P("gx", "gy", "gz", None),
            P("gx", "gy", "gz"),
            P("gx", "gy", "gz"),
            P("gx", "gy", "gz"),
        ),
        out_specs=(P("gx", "gy", "gz"), P("gx", "gy", "gz")),
        check_vma=False,
    )
```

profile of v0, /device:TPU:0, one launch (start us, length us, event | category | flops | bytes accessed | tf_op | source)
XLA Modules:
  0.0 190.4 jit_solution(3773399230261475277)
XLA Ops:
  1.3 0.9 convert_reduce_fusion
  2.2 0.7 multiply_add_fusion.2
  2.9 0.1 compare_and_fusion
  3.0 0.8 fusion.27
  3.7 0.7 copy.32
  4.5 4.3 %all-to-all-start = ((f32[4,1,2]{2,1,0:T(1,128)}), f32[4,1,2]{2,1,0:T(1,128)S(1)}, u32[]{:S(2)}, u32[]{:S(2)}) async-start(f32[4,1,2]{2,1,0:T(1,128)} %copy.32), calls=%async_computation | async-start | bytes 4096 | tf_op jit(solution)/shard_map/all_to_all | solution.py:71
  8.7 2.7 %fusion.17 = f32[4,2,16384]{2,1,0:T(2,128)} fusion(f32[1,1,1,6,16384]{4,2,3,1,0:T(1,128)} %param.6, pred[4,2,6]{2,0,1:T(4,128)(4,1)S(1)} %compare_and_fusion), kind=kOutput, calls=%fused_computation.53 | convolution fusion | flops 9437184 | bytes 917552 | tf_op jit(solution)/shard_map/dot_general | solution.py:66
  11.4 1.0 all-to-all-done
  12.4 3.5 %all-to-all-start.1 = ((f32[4,2,16384]{2,1,0:T(2,128)}), f32[4,2,16384]{2,1,0:T(2,128)S(1)}, u32[]{:S(2)}, u32[]{:S(2)}) async-start(f32[4,2,16384]{2,1,0:T(2,128)} %fusion.17), calls=%async_computation.1 | async-start | bytes 1048576 | tf_op jit(solution)/shard_map/all_to_all | solution.py:68
  15.9 0.5 broadcast.78
  16.4 0.7 reduce.3
  17.1 0.1 eq.63
  17.2 7.5 %all-to-all-done.1 = f32[4,2,16384]{2,1,0:T(2,128)S(1)} async-done(((f32[4,2,16384]{2,1,0:T(2,128)}), f32[4,2,16384]{2,1,0:T(2,128)S(1)}, u32[]{:S(2)}, u32[]{:S(2)}) %all-to-all-start.1) | async-done | bytes 524320 | tf_op jit(solution)/shard_map/all_to_all | solution.py:68
  24.7 0.4 reshape.94
  25.1 5.3 %copy.34 = f32[16384,8]{1,0:T(8,128)} copy(f32[16384,8]{0,1:T(8,128)S(1)} %bitcast.29) | data formatting | bytes 1048576 | tf_op jit(solution)/shard_map/dot_general | solution.py:78
  30.3 15.2 %fusion.2 = f32[32,64,64]{2,0,1:T(8,128)S(1)} fusion(f32[64,2,64,2,8]{4,3,2,1,0:T(2,128)} %bitcast.27, f32[32]{0:T(128)S(1)} %add_convert_fusion, f32[8]{0:T(128)S(1)} %eq.63), kind=kOutput, calls=%fused_computation.2 | convolution fusion | flops 50725120 | bytes 1048736 | tf_op jit(solution)/shard_map/dot_general | solution.py:78
  45.5 0.0 copy-start
  45.5 0.1 broadcast_multiply_fusion
  45.6 0.6 copy.36
  46.2 0.8 copy.37
  47.1 0.6 reshape.95
  47.7 0.1 add.84
  47.7 1.4 collective-permute-start.1
  49.2 1.3 collective-permute-start
  50.5 0.0 collective-permute-done.1
  50.5 2.3 %collective-permute-done = f32[1,64,128]{2,1,0:T(8,128)S(1)} collective-permute-done((f32[1,64,128]{2,1,0:T(8,128)S(1)}, f32[1,64,128]{2,1,0:T(8,128)S(1)}, u32[]{:S(2)}, u32[]{:S(2)}) %collective-permute-start) | collective-permute-done | bytes 32800 | tf_op jit(solution)/shard_map/ppermute | solution.py:21
  52.8 3.9 %collective-permute-start.3 = (f32[18,1,128]{2,1,0:T(1,128)S(1)}, f32[18,1,128]{2,1,0:T(1,128)S(1)}, u32[]{:S(2)}, u32[]{:S(2)}) collective-permute-start(f32[18,1,128]{2,1,0:T(1,128)S(1)} %get-tuple-element.18), channel_id=1, source_target_pairs={{0,2},{2,4},{4,6},{1,3},{3,5},{5,7},{8,10},{10,12},{12,14},{9,11},... | collective-permute-start | bytes 27656 | tf_op jit(solution)/shard_map/ppermute | solution.py:19
  56.7 1.3 collective-permute-start.2
  58.0 0.1 collective-permute-done.3
  58.0 4.2 %collective-permute-done.2 = f32[18,1,128]{2,1,0:T(1,128)S(1)} collective-permute-done((f32[18,1,128]{2,1,0:T(1,128)S(1)}, f32[18,1,128]{2,1,0:T(1,128)S(1)}, u32[]{:S(2)}, u32[]{:S(2)}) %collective-permute-start.2) | collective-permute-done | bytes 9248 | tf_op jit(solution)/shard_map/ppermute | solution.py:21
  62.2 0.1 pad_maximum_fusion
  62.3 0.2 fusion.33
  62.5 0.3 copy.38
  62.8 1.5 collective-permute-start.4
  64.3 0.3 copy.40
  64.6 4.5 %collective-permute-start.5 = (f32[18,66,1]{1,2,0:T(1,128)S(1)}, f32[18,66,1]{1,2,0:T(1,128)S(1)}, u32[]{:S(2)}, u32[]{:S(2)}) collective-permute-start(f32[18,66,1]{1,2,0:T(1,128)S(1)} %copy.40), channel_id=1, source_target_pairs={{0,1},{2,3},{4,5},{6,7},{8,9},{10,11},{12,13},{14,15},{16,17},{18,... | collective-permute-start | bytes 14264 | tf_op jit(solution)/shard_map/ppermute | solution.py:19
  69.1 0.0 collective-permute-done.4
  69.1 0.3 copy.39
  69.5 1.0 collective-permute-done.5
  70.5 0.3 copy.41
  70.8 1.2 multiply_reduce_fusion.2
  72.1 42.5 %all-reduce.1 = (f32[]{:T(128)}, f32[]{:T(128)}) all-reduce(f32[]{:T(128)} %get-tuple-element.5, f32[]{:T(128)} %get-tuple-element.4), channel_id=1, replica_groups=mesh['gx'=4,'gy'=4,'gz'=2] {'gx','gy','gz'}, use_global_device_ids=true, to_apply=%region_3.0 | all-reduce | flops 2 | bytes 16 | tf_op jit(solution)/shard_map/psum | solution.py:44
  115.8 0.1 multiply_subtract_fusion.1
  115.9 1.3 collective-permute-start.7
  117.2 1.3 collective-permute-start.6
  118.5 0.0 collective-permute-done.7
  118.5 4.6 %collective-permute-done.6 = f32[1,64,128]{2,1,0:T(8,128)S(1)} collective-permute-done((f32[1,64,128]{2,1,0:T(8,128)S(1)}, f32[1,64,128]{2,1,0:T(8,128)S(1)}, u32[]{:S(2)}, u32[]{:S(2)}) %collective-permute-start.6) | collective-permute-done | bytes 32800 | tf_op jit(solution)/shard_map/ppermute | solution.py:21
  123.1 2.2 %collective-permute-start.9 = (f32[18,1,128]{2,1,0:T(1,128)S(1)}, f32[18,1,128]{2,1,0:T(1,128)S(1)}, u32[]{:S(2)}, u32[]{:S(2)}) collective-permute-start(f32[18,1,128]{2,1,0:T(1,128)S(1)} %get-tuple-element.16), channel_id=1, source_target_pairs={{0,2},{2,4},{4,6},{1,3},{3,5},{5,7},{8,10},{10,12},{12,14},{9,11},... | collective-permute-start | bytes 27656 | tf_op jit(solution)/shard_map/ppermute | solution.py:19
  125.3 1.3 collective-permute-start.8
  126.6 0.1 collective-permute-done.9
  126.6 4.2 %collective-permute-done.8 = f32[18,1,128]{2,1,0:T(1,128)S(1)} collective-permute-done((f32[18,1,128]{2,1,0:T(1,128)S(1)}, f32[18,1,128]{2,1,0:T(1,128)S(1)}, u32[]{:S(2)}, u32[]{:S(2)}) %collective-permute-start.8) | collective-permute-done | bytes 9248 | tf_op jit(solution)/shard_map/ppermute | solution.py:21
  130.8 0.1 pad_maximum_fusion.1
  130.9 0.2 fusion.32
  131.1 0.3 copy.42
  131.4 1.3 collective-permute-start.10
  132.7 0.3 copy.44
  133.0 4.5 %collective-permute-start.11 = (f32[18,66,1]{1,2,0:T(1,128)S(1)}, f32[18,66,1]{1,2,0:T(1,128)S(1)}, u32[]{:S(2)}, u32[]{:S(2)}) collective-permute-start(f32[18,66,1]{1,2,0:T(1,128)S(1)} %copy.44), channel_id=1, source_target_pairs={{0,1},{2,3},{4,5},{6,7},{8,9},{10,11},{12,13},{14,15},{16,17},{18,... | collective-permute-start | bytes 14264 | tf_op jit(solution)/shard_map/ppermute | solution.py:19
  137.5 0.0 collective-permute-done.10
  137.5 0.3 copy.43
  137.9 1.0 collective-permute-done.11
  138.9 0.3 copy.45
  139.2 2.1 %multiply_reduce_fusion = (f32[]{:T(128)}, f32[]{:T(128)}, f32[16,64,128]{2,1,0:T(8,128)}) fusion(f32[16,64,128]{2,1,0:T(8,128)S(1)} %multiply_subtract_fusion.1, f32[18,1,128]{2,1,0:T(1,128)S(1)} %collective-permute-done.8, f32[1,64,128]{2,1,0:T(8,128)S(1)} %collective-permute-done.6, f32[1,64,128]{2,1,0:T(8,128)S(1)} %collective-permute-done.7, ...), kind=kLoop, calls=%fused_computation.58 | loop fusion | flops 3932158 | bytes 1666344 | tf_op jit(solution)/shard_map/reduce_sum | solution.py:44
  141.3 42.5 %all-reduce = (f32[]{:T(128)}, f32[]{:T(128)}) all-reduce(f32[]{:T(128)} %get-tuple-element.3, f32[]{:T(128)} %get-tuple-element.2), channel_id=1, replica_groups=mesh['gx'=4,'gy'=4,'gz'=2] {'gx','gy','gz'}, use_global_device_ids=true, to_apply=%region_7.0 | all-reduce | flops 2 | bytes 16 | tf_op jit(solution)/shard_map/psum | solution.py:44
  188.2 2.2 %multiply_subtract_fusion = (f32[16,64,128]{2,1,0:T(8,128)}, f32[16,64,128]{2,1,0:T(8,128)}) fusion(f32[16,64,128]{2,1,0:T(8,128)S(1)} %multiply_subtract_fusion.1, f32[16,64,128]{2,1,0:T(8,128)} %get-tuple-element.10, f32[16,64,128]{2,1,0:T(8,128)S(1)} %get-tuple-element.11, f32[]{:T(128)S(6)} %div.13, f32[]{:T(128)S(6)} %div.15, ...), kind=kLoop, calls=%fused_computation.56 | loop fusion | flops 1179648 | bytes 3145740 | tf_op jit(solution)/shard_map/sub | solution.py:93
  (10 shorter events, 0.1 us)
Async XLA Ops:
  4.5 8.0 %all-to-all-start = ((f32[4,1,2]{2,1,0:T(1,128)}), f32[4,1,2]{2,1,0:T(1,128)S(1)}, u32[]{:S(2)}, u32[]{:S(2)}) async-start(f32[4,1,2]{2,1,0:T(1,128)} %copy.32), calls=%async_computation | async-start | bytes 4096 | tf_op jit(solution)/shard_map/all_to_all | solution.py:71
  12.4 12.3 %all-to-all-start.1 = ((f32[4,2,16384]{2,1,0:T(2,128)}), f32[4,2,16384]{2,1,0:T(2,128)S(1)}, u32[]{:S(2)}, u32[]{:S(2)}) async-start(f32[4,2,16384]{2,1,0:T(2,128)} %fusion.17), calls=%async_computation.1 | async-start | bytes 1048576 | tf_op jit(solution)/shard_map/all_to_all | solution.py:68
  30.3 17.3 %copy-start.1 = (f32[16,64,128]{2,1,0:T(8,128)S(1)}, f32[16,64,128]{2,1,0:T(8,128)}, u32[]{:S(2)}) copy-start(f32[16,64,128]{2,1,0:T(8,128)} %param.10) | copy-start | bytes 1572868
  45.5 25.3 %copy-start = (f32[16,64,128]{2,1,0:T(8,128)S(1)}, f32[16,64,128]{2,1,0:T(8,128)}, u32[]{:S(2)}) copy-start(f32[16,64,128]{2,1,0:T(8,128)} %param.11) | copy-start | bytes 1572868
  47.7 2.8 %collective-permute-start.1 = (f32[1,64,128]{2,1,0:T(8,128)S(1)}, f32[1,64,128]{2,1,0:T(8,128)S(1)}, u32[]{:S(2)}, u32[]{:S(2)}) collective-permute-start(f32[1,64,128]{2,1,0:T(8,128)S(1)} %get-tuple-element.24), channel_id=1, source_target_pairs={{0,8},{8,16},{16,24},{1,9},{9,17},{17,25},{2,10},{10,18},{18,26},{... | collective-permute-start | bytes 98312 | tf_op jit(solution)/shard_map/ppermute | solution.py:19
  49.2 3.6 %collective-permute-start = (f32[1,64,128]{2,1,0:T(8,128)S(1)}, f32[1,64,128]{2,1,0:T(8,128)S(1)}, u32[]{:S(2)}, u32[]{:S(2)}) collective-permute-start(f32[1,64,128]{2,1,0:T(8,128)S(1)} %get-tuple-element.25), channel_id=1, source_target_pairs={{8,0},{16,8},{24,16},{9,1},{17,9},{25,17},{10,2},{18,10},{26,18},{... | collective-permute-start | bytes 98312 | tf_op jit(solution)/shard_map/ppermute | solution.py:21
  52.8 5.3 %collective-permute-start.3 = (f32[18,1,128]{2,1,0:T(1,128)S(1)}, f32[18,1,128]{2,1,0:T(1,128)S(1)}, u32[]{:S(2)}, u32[]{:S(2)}) collective-permute-start(f32[18,1,128]{2,1,0:T(1,128)S(1)} %get-tuple-element.18), channel_id=1, source_target_pairs={{0,2},{2,4},{4,6},{1,3},{3,5},{5,7},{8,10},{10,12},{12,14},{9,11},... | collective-permute-start | bytes 27656 | tf_op jit(solution)/shard_map/ppermute | solution.py:19
  56.7 5.6 %collective-permute-start.2 = (f32[18,1,128]{2,1,0:T(1,128)S(1)}, f32[18,1,128]{2,1,0:T(1,128)S(1)}, u32[]{:S(2)}, u32[]{:S(2)}) collective-permute-start(f32[18,1,128]{2,1,0:T(1,128)S(1)} %get-tuple-element.19), channel_id=1, source_target_pairs={{2,0},{4,2},{6,4},{3,1},{5,3},{7,5},{10,8},{12,10},{14,12},{11,9},... | collective-permute-start | bytes 27656 | tf_op jit(solution)/shard_map/ppermute | solution.py:21
  62.8 6.3 %collective-permute-start.4 = (f32[18,66,1]{1,2,0:T(1,128)S(1)}, f32[18,66,1]{1,2,0:T(1,128)S(1)}, u32[]{:S(2)}, u32[]{:S(2)}) collective-permute-start(f32[18,66,1]{1,2,0:T(1,128)S(1)} %copy.38), channel_id=1, source_target_pairs={{1,0},{3,2},{5,4},{7,6},{9,8},{11,10},{13,12},{15,14},{17,16},{19,... | collective-permute-start | bytes 14264 | tf_op jit(solution)/shard_map/ppermute | solution.py:21
  64.6 5.9 %collective-permute-start.5 = (f32[18,66,1]{1,2,0:T(1,128)S(1)}, f32[18,66,1]{1,2,0:T(1,128)S(1)}, u32[]{:S(2)}, u32[]{:S(2)}) collective-permute-start(f32[18,66,1]{1,2,0:T(1,128)S(1)} %copy.40), channel_id=1, source_target_pairs={{0,1},{2,3},{4,5},{6,7},{8,9},{10,11},{12,13},{14,15},{16,17},{18,... | collective-permute-start | bytes 14264 | tf_op jit(solution)/shard_map/ppermute | solution.py:19
  115.9 2.6 %collective-permute-start.7 = (f32[1,64,128]{2,1,0:T(8,128)S(1)}, f32[1,64,128]{2,1,0:T(8,128)S(1)}, u32[]{:S(2)}, u32[]{:S(2)}) collective-permute-start(f32[1,64,128]{2,1,0:T(8,128)S(1)} %get-tuple-element.22), channel_id=1, source_target_pairs={{0,8},{8,16},{16,24},{1,9},{9,17},{17,25},{2,10},{10,18},{18,26},{... | collective-permute-start | bytes 98312 | tf_op jit(solution)/shard_map/ppermute | solution.py:19
  117.2 5.9 %collective-permute-start.6 = (f32[1,64,128]{2,1,0:T(8,128)S(1)}, f32[1,64,128]{2,1,0:T(8,128)S(1)}, u32[]{:S(2)}, u32[]{:S(2)}) collective-permute-start(f32[1,64,128]{2,1,0:T(8,128)S(1)} %get-tuple-element.23), channel_id=1, source_target_pairs={{8,0},{16,8},{24,16},{9,1},{17,9},{25,17},{10,2},{18,10},{26,18},{... | collective-permute-start | bytes 98312 | tf_op jit(solution)/shard_map/ppermute | solution.py:21
  123.1 3.5 %collective-permute-start.9 = (f32[18,1,128]{2,1,0:T(1,128)S(1)}, f32[18,1,128]{2,1,0:T(1,128)S(1)}, u32[]{:S(2)}, u32[]{:S(2)}) collective-permute-start(f32[18,1,128]{2,1,0:T(1,128)S(1)} %get-tuple-element.16), channel_id=1, source_target_pairs={{0,2},{2,4},{4,6},{1,3},{3,5},{5,7},{8,10},{10,12},{12,14},{9,11},... | collective-permute-start | bytes 27656 | tf_op jit(solution)/shard_map/ppermute | solution.py:19
  125.3 5.6 %collective-permute-start.8 = (f32[18,1,128]{2,1,0:T(1,128)S(1)}, f32[18,1,128]{2,1,0:T(1,128)S(1)}, u32[]{:S(2)}, u32[]{:S(2)}) collective-permute-start(f32[18,1,128]{2,1,0:T(1,128)S(1)} %get-tuple-element.17), channel_id=1, source_target_pairs={{2,0},{4,2},{6,4},{3,1},{5,3},{7,5},{10,8},{12,10},{14,12},{11,9},... | collective-permute-start | bytes 27656 | tf_op jit(solution)/shard_map/ppermute | solution.py:21
  131.4 6.1 %collective-permute-start.10 = (f32[18,66,1]{1,2,0:T(1,128)S(1)}, f32[18,66,1]{1,2,0:T(1,128)S(1)}, u32[]{:S(2)}, u32[]{:S(2)}) collective-permute-start(f32[18,66,1]{1,2,0:T(1,128)S(1)} %copy.42), channel_id=1, source_target_pairs={{1,0},{3,2},{5,4},{7,6},{9,8},{11,10},{13,12},{15,14},{17,16},{19,... | collective-permute-start | bytes 14264 | tf_op jit(solution)/shard_map/ppermute | solution.py:21
  133.0 5.9 %collective-permute-start.11 = (f32[18,66,1]{1,2,0:T(1,128)S(1)}, f32[18,66,1]{1,2,0:T(1,128)S(1)}, u32[]{:S(2)}, u32[]{:S(2)}) collective-permute-start(f32[18,66,1]{1,2,0:T(1,128)S(1)} %copy.44), channel_id=1, source_target_pairs={{0,1},{2,3},{4,5},{6,7},{8,9},{10,11},{12,13},{14,15},{16,17},{18,... | collective-permute-start | bytes 14264 | tf_op jit(solution)/shard_map/ppermute | solution.py:19
where the time goes:
time: 191 us; the launch traced here: 190 us
  blocking collectives  84.9 us (44%)
  starting transfers between devices  33.5 us (18%)
  waiting for transfers between devices  25.9 us (14%)
  matrix products  18.6 us (10%)
  local copies, waits for them, and re-layouts  11.9 us (6%)
  other arithmetic  8.21 us (4%)
  between operations  7.33 us (4%)
    psum x2, blocking collectives, paired(): lax.psum((jnp.sum(residual * residual), jnp.sum(residual * image)), ('gx'...  84.9 us
    ppermute x6, starting transfers between devices, padded_2(): lax.ppermute(tail, axis, [(i, (i + 1) % count) for i in range(ends)])  17.9 us
    ppermute x6, waiting for transfers between devices, padded_2(): lax.ppermute(head, axis, [((i + 1) % count, i) for i in range(ends)])  15.2 us
    dot_general x1, matrix products, per_device(): tile_sums = jnp.dot(placing, incoming, precision=lax.Precision.HIGHEST)  15.2 us
    ppermute x6, starting transfers between devices, padded_2(): lax.ppermute(head, axis, [((i + 1) % count, i) for i in range(ends)])  7.94 us
    all_to_all x1, waiting for transfers between devices, per_device(): lax.all_to_all(packed.reshape(group_size, CAP, -1), 'gx', split_axis=0, c...  7.51 us
    dot_general x1, local copies, waits for them, and re-layouts, per_device(): tile_sums = jnp.dot(placing, incoming, precision=lax.Precision.HIGHEST)  5.26 us
    all_to_all x1, starting transfers between devices, per_device(): lax.all_to_all(labels, 'gx', split_axis=0, concat_axis=0, tiled=True)  4.26 us
  transfers between devices with their start and end apart: 14, of which 10 were waited for; matrix products, arithmetic and copies ran while one was open for 3% of the time, Pallas kernels for 0%

commit v1 on v0

v1 whole, which is shorter than its diff:
```python
import functools

import jax
import jax.numpy as jnp
from jax import lax
from jax.experimental import pallas as pl
from jax.experimental.pallas import tpu as pltpu
from jax.sharding import PartitionSpec as P

CAP = 2
AXES = ("gx", "gy", "gz")
TAGS = 8
F32 = jnp.float32
VMEM = pl.BlockSpec(memory_space=pltpu.VMEM)
SMEM = pl.BlockSpec(memory_space=pltpu.SMEM)
S0, S1, V0, V1, V2, U0, U1, U2, E0, E1, SIG = range(11)
CORNER = 16
PAIRS = [(dx, dy, 0) for dx in (-1, 1) for dy in (-1, 1)]
PAIRS += [(dx, 0, dz) for dx in (-1, 1) for dz in (-1, 1)]
PAIRS += [(0, dy, dz) for dy in (-1, 1) for dz in (-1, 1)]


def params(mib=8):
    return pltpu.CompilerParams(vmem_limit_bytes=mib * 1024 * 1024)


def matchings(n):
    first = [(i, i ^ 1) for i in range(n) if (i ^ 1) < n]
    second = [(i, ((i + 1) ^ 1) - 1) for i in range(n) if 0 <= ((i + 1) ^ 1) - 1 < n]
    return [m for m in (first, second) if m]


def peer(i, k, n):
    return i ^ k if n & (n - 1) == 0 else (i + k) % n


def relative(owner, me, n):
    return owner ^ me if n & (n - 1) == 0 else lax.rem(owner - me + n, n)


def iotas(rows, lanes=128):
    shape = (rows, lanes)
    return lax.broadcasted_iota(jnp.int32, shape, 0), lax.broadcasted_iota(jnp.int32, shape, 1)


def roll(x, shift, axis):
    shift = shift % x.shape[axis]
    return x if shift == 0 else pltpu.roll(x, shift, axis)


def total(x):
    return jnp.sum(jnp.sum(x, axis=0, keepdims=True), axis=1, keepdims=True)


def fold(x):
    parts = [x[i : i + 8] for i in range(0, x.shape[0], 8)]
    while len(parts) > 1:
        rest = parts[len(parts) // 2 * 2 :]
        parts = [parts[i] + parts[i + 1] for i in range(0, len(parts) - 1, 2)] + rest
    return parts[0]


def flags(axis, n):
    at = lax.axis_index(axis)
    odd = lax.rem(at, 2) == 1
    low = jnp.where(at > 0, 1.0, 0.0).astype(F32)
    high = jnp.where(at < n - 1, 1.0, 0.0).astype(F32)
    return odd, low, high


def pick(odd, first, second):
    if second is None:
        return first, first
    return jnp.where(odd, first, second), jnp.where(odd, second, first)


def pack_kernel(n, owner_ref, tile_ref, live_ref, blocks_ref, out_ref):
    count, side = blocks_ref.shape[0], blocks_ref.shape[1]
    half = side // 2
    me = lax.axis_index("gx")
    live = live_ref[0]
    src, dst = iotas(side, side)
    gather = jnp.where(src // 2 == dst % half, 0.25, 0.0).astype(jnp.bfloat16)
    out_ref[...] = jnp.zeros_like(out_ref)
    _, lane = iotas(half)
    _, lane_t = iotas(TAGS)
    for i in range(count):
        rows = blocks_ref[i, pl.ds(0, half, 2), :] + blocks_ref[i, pl.ds(1, half, 2), :]
        a = rows.astype(jnp.bfloat16)
        rest = rows - a.astype(F32)
        b = rest.astype(jnp.bfloat16)
        c = (rest - b.astype(F32)).astype(jnp.bfloat16)
        both = sum(jnp.dot(p, gather, preferred_element_type=F32) for p in (c, b, a))
        owner = owner_ref[i]
        slot = jnp.int32(0)
        for j in range(i):
            slot = slot + jnp.where(owner_ref[j] == owner, 1, 0)
        tag = jnp.where(i < live, tile_ref[i] + 1, 0).astype(F32)
        to = relative(owner, me, n)
        old = out_ref[pl.ds(to, 1), 0:half, :][0]
        new = jnp.where(lane // half == slot, both, old)
        out_ref[pl.ds(to, 1), 0:half, :] = new[None]
        old = out_ref[pl.ds(to, 1), half : half + TAGS, :][0]
        new = jnp.where(lane_t // half == slot, tag, old)
        out_ref[pl.ds(to, 1), half : half + TAGS, :] = new[None]


def local_operator(layer, x, count, here, diag, row, lane):
    rows = here.shape[0]
    beside = jnp.where(row == 0, 0.0, roll(here, 1, 0)) + jnp.where(
        row == rows - 1, 0.0, roll(here, -1, 0)
    )
    beside = beside + jnp.where(lane == 0, 0.0, roll(here, 1, 1))
    beside = beside + jnp.where(lane == 127, 0.0, roll(here, -1, 1))
    if x > 0:
        beside = beside + layer(x - 1)
    if x < count - 1:
        beside = beside + layer(x + 1)
    return (6.0 + diag) * here - beside


def load_kernel(sizes, dims, *refs):
    nx, ny, nz = sizes
    X, Y = dims
    chunks, (rhs_ref, diag_ref), rest = refs[:nx], refs[nx : nx + 2], refs[nx + 2 :]
    r_ref, pw_ref = rest[:2]
    face_refs, turned = rest[2:-1], rest[-1]
    row, lane = iotas(Y)
    half = Y
    _, lane1 = iotas(1)
    tags = []
    for k, ref in enumerate(chunks):
        turned[k * Y : (k + 1) * Y, :] = roll(ref[0:half, :], half, 1)
        tag = ref[half : half + 1, :]
        tags.append((tag, roll(tag, half, 1)))
    for x in range(X):
        want = (2 * x + 1 + lane1 // half).astype(F32)
        acc = rhs_ref[x * Y : (x + 1) * Y, :]
        for k, ref in enumerate(chunks):
            straight, swapped = tags[k]
            acc = acc + jnp.where(straight == want, ref[0:half, :], 0.0)
            acc = acc + jnp.where(swapped == want, turned[k * Y : (k + 1) * Y, :], 0.0)
        r_ref[x * Y : (x + 1) * Y, :] = acc

    def layer(x):
        return r_ref[x * Y : (x + 1) * Y, :]

    tile = jnp.zeros((Y, 128), F32)
    for x in range(X):
        here = layer(x)
        pw = local_operator(layer, x, X, here, diag_ref[x * Y : (x + 1) * Y, :], row, lane)
        pw_ref[x * Y : (x + 1) * Y, :] = pw
        tile = jnp.where(lane // 2 == x, roll(here, 2 * x + 1, 1), tile)
        tile = jnp.where(lane // 2 == X + x, roll(pw, 2 * (X + x) + 1, 1), tile)
    faces = iter(face_refs)
    odd, _, _ = flags("gx", nx)
    for m in range(len(matchings(nx))):
        top = jnp.where(odd, 0, (X - 1) * Y) if m == 0 else jnp.where(odd, (X - 1) * Y, 0)
        top = pl.multiple_of(top, Y)
        out = next(faces)
        out[0:Y, :] = r_ref[pl.ds(top, Y), :]
        out[Y : 2 * Y, :] = pw_ref[pl.ds(top, Y), :]
    odd, _, _ = flags("gy", ny)
    for m in range(len(matchings(ny))):
        out = next(faces)
        for j, ref in enumerate((r_ref, pw_ref)):
            low, high = ref[pl.ds(0, X, Y), :], ref[pl.ds(Y - 1, X, Y), :]
            out[j * X : (j + 1) * X, :] = jnp.where(odd, low, high) if m == 0 else jnp.where(
                odd, high, low
            )
    next(faces)[...] = tile


def moment_kernel(sizes, dims, *refs):
    nx, ny, nz = sizes
    X, Y = dims
    refs = list(refs)
    r_ref, pw_ref, diag_ref, tile_ref = refs[:4]
    refs = refs[4:]

    def received(n):
        got = [refs.pop(0) for _ in matchings(n)]
        return got + [None] * (2 - len(got))

    fx, fy, fz = received(nx), received(ny), received(nz)
    w_ref, s_ref, pay_ref, hw_ref = refs
    row, lane = iotas(Y)
    _, lane1 = iotas(1)

    def faces(got, axis, n, a, b):
        odd, low, high = flags(axis, n)
        if not [g for g in got if g is not None]:
            return jnp.zeros((b - a, 128), F32), jnp.zeros((b - a, 128), F32), low, high
        one, two = [None if g is None else g[a:b, :] for g in got]
        lo, hi = pick(odd, one, two)
        return lo * low, hi * high, low, high

    xlr, xhr, x_low, x_high = faces(fx, "gx", nx, 0, Y)
    xlp, xhp, _, _ = faces(fx, "gx", nx, Y, 2 * Y)
    ylr, yhr, y_low, y_high = faces(fy, "gy", ny, 0, X)
    ylp, yhp, _, _ = faces(fy, "gy", ny, X, 2 * X)
    zl, zh, z_low, z_high = faces(fz, "gz", nz, 0, Y)
    zt = jnp.where(lane % 2 == 0, roll(zh, -1, 1), roll(zl, 1, 1))
    zflag = jnp.where(lane1 == 0, z_low, jnp.where(lane1 == 127, z_high, 0.0))

    acc = {k: jnp.zeros((8, 128), F32) for k in (S0, S1, V0, V1, V2, U0, U1, U2, E0, E1)}

    def add(key, value):
        acc[key] = acc[key] + fold(value)

    for x in range(X):
        zr_all = roll(zt, -(2 * x + 1), 1)
        zp_all = roll(zt, -(2 * (X + x) + 1), 1)
        for lo, hi in ((0, 8), (8, Y - 8), (Y - 8, Y)):
            sl = slice(x * Y + lo, x * Y + hi)
            r, pw = r_ref[sl, :], pw_ref[sl, :]
            on_z = jnp.where((lane == 0) | (lane == 127), zflag, 0.0)[lo:hi]
            zr = jnp.where(on_z > 0.0, zr_all[lo:hi], 0.0)
            zw = jnp.where(on_z > 0.0, zp_all[lo:hi] - r, 0.0)
            hr, hw, hp, h2, n = zr, zw, zw * zr, zr * zr, on_z
            edge = False
            if lo == 0 or hi == Y:
                edge = True
                at = row[lo:hi] == (0 if lo == 0 else Y - 1)
                fr, fp, flag = (ylr, ylp, y_low) if lo == 0 else (yhr, yhp, y_high)
                yr = jnp.where(at, fr[x : x + 1], 0.0)
                yw = jnp.where(at, (fp[x : x + 1] - r) * flag, 0.0)
                hr, hw, hp, h2 = hr + yr, hw + yw, hp + yw * yr, h2 + yr * yr
                n = n + jnp.where(at, flag, 0.0)
            for end, fr, fp, flag in ((0, xlr, xlp, x_low), (X - 1, xhr, xhp, x_high)):
                if x == end:
                    edge = True
                    xr = fr[lo:hi]
                    xw = (fp[lo:hi] - r) * flag
                    hr, hw, hp, h2 = hr + xr, hw + xw, hp + xw * xr, h2 + xr * xr
                    n = n + flag
            w = pw - hr
            w_ref[sl, :] = w
            hw_ref[sl, :] = hw
            add(S0, r * r)
            add(S1, r * w)
            if edge:
                add(E0, hr * hr - h2)
                add(E1, hw * hr - hp - (n - 1.0) * r * hr)

    s0, s1 = total(acc[S0]), total(acc[S1])
    sigma = jnp.where(s1 > 0.0, s0 / jnp.where(s1 > 0.0, s1, 1.0), 0.15)
    sigma = jnp.clip(sigma, 0.05, 20.0)

    def layer(x):
        return w_ref[x * Y : (x + 1) * Y, :]

    for x in range(X):
        sl = slice(x * Y, (x + 1) * Y)
        w, r = layer(x), r_ref[sl, :]
        s = local_operator(layer, x, X, w, diag_ref[sl, :], row, lane) - hw_ref[sl, :]
        s_ref[sl, :] = s
        sw = sigma * w
        v = r - sw
        u = w - sigma * s
        add(V0, v * v)
        add(V1, v * w)
        add(V2, w * w)
        add(U0, v * u)
        add(U1, (v - sw) * s + w * w)
        add(U2, w * s)

    mom = jnp.where(lane1 == SIG, sigma, 0.0)
    for k, part in acc.items():
        value = s0 if k == S0 else s1 if k == S1 else total(part)
        mom = jnp.where(lane1 == k, value, mom)
    for j in range(4):
        at = (X - 1 if j // 2 else 0) * Y + (Y - 1 if j % 2 else 0)
        mom = jnp.where(lane1 // 2 == CORNER // 2 + j, roll(r_ref[at : at + 1, :], CORNER + 2 * j + 1, 1), mom)
    count = pay_ref.shape[0]
    parity, _ = iotas(count)
    pay_ref[...] = jnp.where(parity % 2 == 0, mom, 0.0)
    tile = tile_ref[...]
    for dx, dy, dz in PAIRS:
        exists, to = neighbour(sizes, dx, dy, dz)
        x, y = (X - 1 if dx > 0 else 0), (Y - 1 if dy > 0 else 0)
        if dz == 0:
            line = r_ref[x * Y + y : x * Y + y + 1, :]
        elif dx == 0:
            line = tile_ref[y : y + 1, :]
        else:
            column = jnp.sum(jnp.where(lane == 2 * x + (0 if dz > 0 else 1), tile, 0.0), axis=1, keepdims=True)
            line = jnp.sum(jnp.where(row == lane, column, 0.0), axis=0, keepdims=True)
        pay_ref[pl.ds(2 * to + 1, 1), :] = line


def neighbour(sizes, dx, dy, dz):
    at = [lax.axis_index(a) for a in AXES]
    to = [p + d for p, d in zip(at, (dx, dy, dz))]
    good = None
    for p, n in zip(to, sizes):
        ok = (p >= 0) & (p < n)
        good = ok if good is None else good & ok
    flat = (to[0] * sizes[1] + to[1]) * sizes[2] + to[2]
    own = (at[0] * sizes[1] + at[1]) * sizes[2] + at[2]
    return jnp.where(good, 1.0, 0.0).astype(F32), jnp.where(good, flat, own)


def final_kernel(sizes, dims, pay_ref, r_ref, w_ref, s_ref, x_out, r_out):
    nx, ny, nz = sizes
    X, Y = dims
    devices = nx * ny * nz
    row, lane = iotas(Y)
    _, lane1 = iotas(1)
    drow, dlane = iotas(devices)
    mom = pay_ref[pl.ds(0, devices, 2), :]

    def column(k):
        return jnp.sum(jnp.where(dlane == k, mom, 0.0), axis=1, keepdims=True)

    def over(x):
        return jnp.sum(x, axis=0, keepdims=True)

    sums = over(mom)

    def lane_of(k):
        return jnp.sum(jnp.where(lane1 == k, sums, 0.0), axis=1, keepdims=True)

    norm0, rw = lane_of(S0), lane_of(S1)
    alpha = norm0 / rw
    delta = column(SIG) - alpha
    v1, v2 = column(V1), column(V2)
    norm1 = over(column(V0) + delta * (2.0 * v1 + delta * v2))
    r1w = over(v1 + delta * v2)
    r1ar1 = over(column(U0) + delta * (column(U1) + delta * column(U2)))
    place = [drow // (ny * nz), (drow // nz) % ny, drow % nz]
    opposite = jnp.zeros((devices, 128), F32)
    for dy in (-1, 1):
        for dz in (-1, 1):
            mine = CORNER + 2 * (2 + (dy > 0)) + (0 if dz > 0 else 1)
            theirs = CORNER + 2 * (0 + (dy < 0)) + (1 if dz > 0 else 0)
            step = (ny + dy) * nz + dz
            ok = (place[0] < nx - 1) & (place[1] + dy >= 0) & (place[1] + dy < ny)
            ok = ok & (place[2] + dz >= 0) & (place[2] + dz < nz) & (dlane == mine)
            other = roll(roll(mom, -step, 0), mine - theirs, 1)
            opposite = opposite + jnp.where(ok, mom * other, 0.0)
    e1 = lane_of(E1) - 12.0 * total(opposite)
    r1ar1 = r1ar1 - alpha * lane_of(E0) + alpha * alpha * e1
    beta = norm1 / norm0
    alpha1 = norm1 / (r1ar1 + beta * (2.0 * r1w + beta * rw))

    xy, xz, yz = {}, {}, {}
    for dx, dy, dz in PAIRS:
        exists, at = neighbour(sizes, dx, dy, dz)
        line = pay_ref[pl.ds(2 * at + 1, 1), :] * (2.0 * exists)
        if dz == 0:
            xy[dx, dy] = line
        elif dx == 0:
            yz[dy, dz] = line
        else:
            xz[dx, dz] = jnp.sum(jnp.where(row == lane, line, 0.0), axis=1, keepdims=True)
    row8, lane8 = iotas(8)
    rim = {}
    for dy in (-1, 1):
        rim[dy] = jnp.where(lane1 % 2 == 0, roll(yz[dy, 1], -1, 1), roll(yz[dy, -1], 1, 1))
    rim = jnp.where(row8 == 0, rim[-1], jnp.where(row8 == 7, rim[1], 0.0))
    sides = (lane8 == 0) | (lane8 == 127)

    for x in range(X):
        turned = jnp.where(sides, roll(rim, -(2 * x + 1), 1), 0.0)
        for lo, hi in ((0, 8), (8, Y - 8), (Y - 8, Y)):
            sl = slice(x * Y + lo, x * Y + hi)
            r, w, s = r_ref[sl, :], w_ref[sl, :], s_ref[sl, :]
            dx = -1 if x == 0 else 1 if x == X - 1 else 0
            dy = -1 if lo == 0 else 1 if hi == Y else 0
            if dy:
                at = row8 == (0 if dy < 0 else 7)
                s = s + jnp.where(at, turned, 0.0)
                if dx:
                    s = s + jnp.where(at, xy[dx, dy], 0.0)
            if dx:
                ln = lane[lo:hi]
                s = s + jnp.where(ln == 0, xz[dx, -1][lo:hi], jnp.where(ln == 127, xz[dx, 1][lo:hi], 0.0))
            r1 = r - alpha * w
            x_out[sl, :] = alpha * r + alpha1 * (r1 + beta * r)
            r_out[sl, :] = r1 - alpha1 * (w - alpha * s + beta * w)


def per_device(face_blocks, owner_rank, owner_tile, live_count, right_side, diagonal):
    sizes = tuple(lax.axis_size(a) for a in AXES)
    nx, ny, nz = sizes
    X, Y, Z = right_side.shape
    dims = (X, Y)
    count = face_blocks.shape[3]
    side = 2 * Y
    flat = jax.ShapeDtypeStruct((X * Y, Z), F32)
    rhs, diag = right_side.reshape(X * Y, Z), diagonal.reshape(X * Y, Z)

    packed = pl.pallas_call(
        functools.partial(pack_kernel, nx),
        out_shape=jax.ShapeDtypeStruct((nx, Y + TAGS, 128), F32),
        in_specs=[SMEM, SMEM, SMEM, VMEM],
        out_specs=VMEM,
        compiler_params=params(),
        name="pack",
    )(
        owner_rank.reshape(count),
        owner_tile.reshape(count),
        live_count.reshape(1),
        face_blocks.reshape(count, side, side),
    )
    chunks = [packed[0]]
    for k in range(1, nx):
        chunks.append(lax.ppermute(packed[k], "gx", [(i, peer(i, k, nx)) for i in range(nx)]))

    def face_shapes():
        shapes = [(2 * Y, Z)] * len(matchings(nx)) + [(2 * X, Z)] * len(matchings(ny)) + [(Y, Z)]
        return [jax.ShapeDtypeStruct(s, F32) for s in shapes]

    r, pw, *faces = pl.pallas_call(
        functools.partial(load_kernel, sizes, dims),
        out_shape=[flat, flat] + face_shapes(),
        in_specs=[VMEM] * (nx + 2),
        out_specs=[VMEM] * (2 + len(face_shapes())),
        scratch_shapes=[pltpu.VMEM((nx * Y, 128), F32)],
        compiler_params=params(),
        name="load",
    )(*chunks, rhs, diag)
    tile = faces[-1]
    got = []
    sent = iter(faces[:-1])
    for axis, n in (("gx", nx), ("gy", ny)):
        for pairs in matchings(n):
            got.append(lax.ppermute(next(sent), axis, pairs))
    for pairs in matchings(nz):
        got.append(lax.ppermute(tile, "gz", pairs))

    w, s, pay = pl.pallas_call(
        functools.partial(moment_kernel, sizes, dims),
        out_shape=[flat, flat, jax.ShapeDtypeStruct((2 * nx * ny * nz, 128), F32)],
        in_specs=[VMEM] * (4 + len(got)),
        out_specs=[VMEM] * 3,
        scratch_shapes=[pltpu.VMEM((X * Y, 128), F32)],
        compiler_params=params(),
        name="moments",
    )(r, pw, diag, tile, *got)
    pay = lax.all_to_all(pay, AXES, split_axis=0, concat_axis=0, tiled=True)
    x2, r2 = pl.pallas_call(
        functools.partial(final_kernel, sizes, dims),
        out_shape=[flat, flat],
        in_specs=[VMEM] * 4,
        out_specs=[VMEM] * 2,
        compiler_params=params(),
        name="final",
    )(pay, r, w, s)
    return x2.reshape(X, Y, Z), r2.reshape(X, Y, Z)


def solution(mesh):
    return jax.shard_map(
        per_device,
        mesh=mesh,
        in_specs=(
            P("gx", "gy", "gz", None, None),
            P("gx", "gy", "gz", None, None),
            P("gx", "gy", "gz", None),
            P("gx", "gy", "gz"),
            P("gx", "gy", "gz"),
            P("gx", "gy", "gz"),
        ),
        out_specs=(P("gx", "gy", "gz"), P("gx", "gy", "gz")),
        check_vma=False,
    )
```

time: 191 us -> 38.5 us (0.20)
  blocking collectives: 84.9 us -> 16.2 us
  starting transfers between devices: 33.5 us -> 7.69 us
  waiting for transfers between devices: 25.9 us -> 4.89 us
  matrix products: 18.6 us -> 0 us
  local copies, waits for them, and re-layouts: 11.9 us -> 3.36 us
  other arithmetic: 8.21 us -> 0 us
  between operations: 7.33 us -> 1.42 us
  Pallas kernels: 0 us -> 4.71 us
    psum x2 -> x0, blocking collectives: 84.9 us -> none  [paired(): lax.psum((jnp.sum(residual * residual), jnp.sum(residual * image)), ('gx'...]
    dot_general x3 -> x0, matrix products: 18.6 us -> none  [the longest x1 15.2 us: per_device(): tile_sums = jnp.dot(placing, incoming, precision=lax.Precision.HIGHEST)]
    ppermute x12 -> x8, starting transfers between devices: 25.8 us -> 7.69 us  [the longest x3 3.17 us: per_device(): lax.ppermute(packed[k], 'gx', [(i, peer(i, k, nx)) for i in range(nx)])]
    all_to_all x0 -> x1, blocking collectives: none -> 16.2 us  [per_device(): pay = lax.all_to_all(pay, AXES, split_axis=0, concat_axis=0, tiled=True)]
    ppermute x12 -> x8, waiting for transfers between devices: 17.3 us -> 4.89 us  [the longest x3 3.38 us: per_device(): lax.ppermute(packed[k], 'gx', [(i, peer(i, k, nx)) for i in range(nx)])]
    all_to_all x2 -> x0, waiting for transfers between devices: 8.53 us -> none  [the longest x1 7.51 us: per_device(): lax.all_to_all(packed.reshape(group_size, CAP, -1), 'gx', split_axis=0, c...]
    all_to_all x2 -> x0, starting transfers between devices: 7.74 us -> none  [the longest x1 4.26 us: per_device(): lax.all_to_all(labels, 'gx', split_axis=0, concat_axis=0, tiled=True)]
    dot_general x1 -> x0, local copies, waits for them, and re-layouts: 5.26 us -> none  [per_device(): tile_sums = jnp.dot(placing, incoming, precision=lax.Precision.HIGHEST)]
  transfers between devices with their start and end apart: 14 -> 8, of which waited for: 10 -> 3; matrix products, arithmetic and copies ran while one was open for 3% -> 0% of each run, Pallas kernels for 0% -> 0%
where the time goes in v1:
time: 38.5 us; the launch traced here: 38.3 us
  blocking collectives  16.2 us (42%)
  starting transfers between devices  7.69 us (20%)
  waiting for transfers between devices  4.89 us (13%)
  Pallas kernels  4.71 us (12%)
  local copies, waits for them, and re-layouts  3.36 us (9%)
  between operations  1.42 us (4%)
    all_to_all x1, blocking collectives, per_device(): pay = lax.all_to_all(pay, AXES, split_axis=0, concat_axis=0, tiled=True)  16.2 us
    ppermute x3, waiting for transfers between devices, per_device(): lax.ppermute(packed[k], 'gx', [(i, peer(i, k, nx)) for i in range(nx)])  3.38 us
    unnamed x10, local copies, waits for them, and re-layouts  3.34 us
    ppermute x3, starting transfers between devices, per_device(): lax.ppermute(packed[k], 'gx', [(i, peer(i, k, nx)) for i in range(nx)])  3.17 us
    ppermute x4, starting transfers between devices, per_device(): got.append(lax.ppermute(next(sent), axis, pairs))  2.96 us
    ppermute x1, starting transfers between devices, per_device(): got.append(lax.ppermute(tile, 'gz', pairs))  1.56 us
    ppermute x4, waiting for transfers between devices, per_device(): got.append(lax.ppermute(next(sent), axis, pairs))  1.51 us
    pallas_call x1, Pallas kernels, per_device(): pl.pallas_call(functools.partial(final_kernel, sizes, dims), out_shape=[f...  1.38 us
  transfers between devices with their start and end apart: 8, of which 3 were waited for; matrix products, arithmetic and copies ran while one was open for 0% of the time, Pallas kernels for 0%

profile of v1, /device:TPU:0, one launch (start us, length us, event | category | flops | bytes accessed | tf_op | source)
XLA Modules:
  0.0 38.3 jit_solution(10336132116983581192)
XLA Ops:
  0.6 0.0 copy-start
  1.3 0.0 copy-start.2
  1.4 1.0 %copy-done.2 = f32[1,1,1,6,16384]{4,2,3,1,0:T(1,128)S(1)} copy-done((f32[1,1,1,6,16384]{4,2,3,1,0:T(1,128)S(1)}, f32[1,1,1,6,16384]{4,2,3,1,0:T(1,128)}, u32[]{:S(2)}) %copy-start.2) | copy-done | bytes 393240
  2.3 0.0 copy-start.3
  2.3 0.7 %copy-done.3 = s32[1,1,1,6,1]{3,4,2,1,0:T(1,128)S(1)} copy-done((s32[1,1,1,6,1]{3,4,2,1,0:T(1,128)S(1)}, s32[1,1,1,6,1]{3,4,2,1,0:T(1,128)}, u32[]{:S(2)}) %copy-start.3) | copy-done | bytes 48
  3.0 0.0 copy-start.4
  3.0 0.7 %copy-done.4 = s32[1,1,1,6]{3,2,1,0:T(1,128)S(1)} copy-done((s32[1,1,1,6]{3,2,1,0:T(1,128)S(1)}, s32[1,1,1,6]{3,2,1,0:T(1,128)}, u32[]{:S(2)}) %copy-start.4) | copy-done | bytes 48
  3.7 0.8 %pack.1 = f32[4,72,128]{2,1,0:T(8,128)S(1)} custom-call(s32[6]{0:T(128)S(1)} %bitcast.25, s32[6]{0:T(128)S(1)} %bitcast.26, s32[1]{0:T(128)} %bitcast.18.live_ref, f32[6,128,128]{2,1,0:T(8,128)S(1)} %bitcast.22), custom_call_target="tpu_custom_call" | custom-call | tf_op jit(solution)/shard_map/pack/pallas_call | solution.py:394
  4.5 2.5 %collective-permute-start.2 = (f32[72,128]{1,0:T(8,128)S(1)}, f32[72,128]{1,0:T(8,128)S(1)}, u32[]{:S(2)}, u32[]{:S(2)}) collective-permute-start(f32[72,128]{1,0:T(8,128)S(1)} %get-tuple-element.26), channel_id=1, source_target_pairs={{0,24},{8,16},{16,8},{24,0},{1,25},{9,17},{17,9},{25,1},{2,26},{10... | collective-permute-start | bytes 110600 | tf_op jit(solution)/shard_map/ppermute | solution.py:409
  7.0 0.6 %collective-permute-start.1 = (f32[72,128]{1,0:T(8,128)S(1)}, f32[72,128]{1,0:T(8,128)S(1)}, u32[]{:S(2)}, u32[]{:S(2)}) collective-permute-start(f32[72,128]{1,0:T(8,128)S(1)} %get-tuple-element.27), channel_id=1, source_target_pairs={{0,16},{8,24},{16,0},{24,8},{1,17},{9,25},{17,1},{25,9},{2,18},{10... | collective-permute-start | bytes 110600 | tf_op jit(solution)/shard_map/ppermute | solution.py:409
  7.7 0.0 collective-permute-start
  7.7 1.2 %collective-permute-done.2.refs_3_ = f32[72,128]{1,0:T(8,128)S(1)} collective-permute-done((f32[72,128]{1,0:T(8,128)S(1)}, f32[72,128]{1,0:T(8,128)S(1)}, u32[]{:S(2)}, u32[]{:S(2)}) %collective-permute-start.2) | collective-permute-done | bytes 36896 | tf_op jit(solution)/shard_map/ppermute | solution.py:409
  8.9 2.2 %collective-permute-done.1.refs_2_ = f32[72,128]{1,0:T(8,128)S(1)} collective-permute-done((f32[72,128]{1,0:T(8,128)S(1)}, f32[72,128]{1,0:T(8,128)S(1)}, u32[]{:S(2)}, u32[]{:S(2)}) %collective-permute-start.1) | collective-permute-done | bytes 36896 | tf_op jit(solution)/shard_map/ppermute | solution.py:409
  11.1 0.0 collective-permute-done.refs_1_
  11.1 0.0 copy-done
  11.1 0.0 copy-start.1
  11.1 1.0 %copy-done.1 = f32[16,64,128]{2,1,0:T(8,128)S(1)} copy-done((f32[16,64,128]{2,1,0:T(8,128)S(1)}, f32[16,64,128]{2,1,0:T(8,128)}, u32[]{:S(2)}) %copy-start.1) | copy-done | bytes 524312
  12.1 1.3 %load.1 = (f32[1024,128]{1,0:T(8,128)S(1)}, f32[1024,128]{1,0:T(8,128)S(1)}, f32[128,128]{1,0:T(8,128)S(1)}, f32[128,128]{1,0:T(8,128)S(1)}, f32[32,128]{1,0:T(8...) custom-call(f32[72,128]{1,0:T(8,128)S(1)} %get-tuple-element.29.refs_0_, ...), custom_call_target="tpu_custom_call" | custom-call | tf_op jit(solution)/shard_map/load/pallas_call | solution.py:415
  13.4 0.1 collective-permute-start.3
  13.5 0.7 %collective-permute-start.4 = (f32[128,128]{1,0:T(8,128)S(1)}, f32[128,128]{1,0:T(8,128)S(1)}, u32[]{:S(2)}, u32[]{:S(2)}) collective-permute-start(f32[128,128]{1,0:T(8,128)S(1)} %get-tuple-element.18), channel_id=1, source_target_pairs={{8,16},{16,8},{9,17},{17,9},{10,18},{18,10},{11,19},{19,11},{12,20... | collective-permute-start | bytes 196616 | tf_op jit(solution)/shard_map/ppermute | solution.py:429
  14.2 1.6 %collective-permute-start.7 = (f32[64,128]{1,0:T(8,128)S(1)}, f32[64,128]{1,0:T(8,128)S(1)}, u32[]{:S(2)}, u32[]{:S(2)}) collective-permute-start(f32[64,128]{1,0:T(8,128)S(1)} %get-tuple-element.16.refs_3_), channel_id=1, source_target_pairs={{0,1},{1,0},{2,3},{3,2},{4,5},{5,4},{6,7},{7,6},{8,9},{9,8},{10,11... | collective-permute-start | bytes 98312 | tf_op jit(solution)/shard_map/ppermute | solution.py:431
  15.7 1.6 %collective-permute-start.5 = (f32[32,128]{1,0:T(8,128)S(1)}, f32[32,128]{1,0:T(8,128)S(1)}, u32[]{:S(2)}, u32[]{:S(2)}) collective-permute-start(f32[32,128]{1,0:T(8,128)S(1)} %get-tuple-element.19), channel_id=1, source_target_pairs={{0,2},{2,0},{4,6},{6,4},{1,3},{3,1},{5,7},{7,5},{8,10},{10,8},{12,... | collective-permute-start | bytes 49160 | tf_op jit(solution)/shard_map/ppermute | solution.py:429
  17.3 0.7 %collective-permute-start.6 = (f32[32,128]{1,0:T(8,128)S(1)}, f32[32,128]{1,0:T(8,128)S(1)}, u32[]{:S(2)}, u32[]{:S(2)}) collective-permute-start(f32[32,128]{1,0:T(8,128)S(1)} %get-tuple-element.20), channel_id=1, source_target_pairs={{2,4},{4,2},{3,5},{5,3},{10,12},{12,10},{11,13},{13,11},{18,20},{2... | collective-permute-start | bytes 49160 | tf_op jit(solution)/shard_map/ppermute | solution.py:429
  18.0 1.5 %collective-permute-done.5.refs_6_ = f32[32,128]{1,0:T(8,128)S(1)} collective-permute-done((f32[32,128]{1,0:T(8,128)S(1)}, f32[32,128]{1,0:T(8,128)S(1)}, u32[]{:S(2)}, u32[]{:S(2)}) %collective-permute-start.5) | collective-permute-done | bytes 16416 | tf_op jit(solution)/shard_map/ppermute | solution.py:429
  19.5 0.0 collective-permute-done.6.refs_7_
  19.5 0.0 collective-permute-done.7.refs_8_
  19.5 0.0 collective-permute-done.3.refs_4_
  19.5 0.0 collective-permute-done.4.refs_5_
  19.5 1.2 %moments.1 = (f32[1024,128]{1,0:T(8,128)S(1)}, f32[1024,128]{1,0:T(8,128)S(1)}, f32[64,128]{1,0:T(8,128)S(1)}) custom-call(f32[1024,128]{1,0:T(8,128)S(1)} %get-tuple-element.14.refs_0_.r_ref, f32[1024,128]{1,0:T(8,128)S(1)} %get-tuple-element.15.refs_1_, f32[1024,128]{1,0:T(8,128)S(1)} %bitcast.20, f32[64,128]{1,0:T(8,128)S(1)} %get-tuple-element.16.refs_3_, ...), custom_call_target="tpu_custom_call" | custom-call | tf_op jit(solution)/shard_map/moments/pallas_call | solution.py:433
  20.7 16.2 %all_to_all.11 = f32[32,2,128]{2,1,0:T(2,128)S(1)} all-to-all(f32[32,2,128]{2,1,0:T(2,128)S(1)} %bitcast.24), channel_id=1, replica_groups=mesh['gx'=4,'gy'=4,'gz'=2] {'gx','gy','gz'}, dimensions={0} | all-to-all | bytes 65536 | tf_op jit(solution)/shard_map/all_to_all | solution.py:442
  36.9 1.4 %final.1 = (f32[1024,128]{1,0:T(8,128)}, f32[1024,128]{1,0:T(8,128)}) custom-call(f32[64,128]{1,0:T(8,128)S(1)} %bitcast.23, f32[1024,128]{1,0:T(8,128)S(1)} %get-tuple-element.14.refs_0_.r_ref, f32[1024,128]{1,0:T(8,128)S(1)} %get-tuple-element.22.w_ref, f32[1024,128]{1,0:T(8,128)S(1)} %get-tuple-element.23.s_ref), custom_call_target="tpu_custom_call" | custom-call | tf_op jit(solution)/shard_map/final/pallas_call | solution.py:443
  (1 shorter events, 0.0 us)
Async XLA Ops:
  0.6 10.4 %copy-start = (f32[16,64,128]{2,1,0:T(8,128)S(1)}, f32[16,64,128]{2,1,0:T(8,128)}, u32[]{:S(2)}) copy-start(f32[16,64,128]{2,1,0:T(8,128)} %param.11) | copy-start | bytes 1572868
  1.3 1.0 %copy-start.2 = (f32[1,1,1,6,16384]{4,2,3,1,0:T(1,128)S(1)}, f32[1,1,1,6,16384]{4,2,3,1,0:T(1,128)}, u32[]{:S(2)}) copy-start(f32[1,1,1,6,16384]{4,2,3,1,0:T(1,128)} %param.6) | copy-start | bytes 1179652
  2.3 0.7 %copy-start.3 = (s32[1,1,1,6,1]{3,4,2,1,0:T(1,128)S(1)}, s32[1,1,1,6,1]{3,4,2,1,0:T(1,128)}, u32[]{:S(2)}) copy-start(s32[1,1,1,6,1]{3,4,2,1,0:T(1,128)} %param.7) | copy-start | bytes 76
  3.0 0.7 %copy-start.4 = (s32[1,1,1,6]{3,2,1,0:T(1,128)S(1)}, s32[1,1,1,6]{3,2,1,0:T(1,128)}, u32[]{:S(2)}) copy-start(s32[1,1,1,6]{3,2,1,0:T(1,128)} %param.8) | copy-start | bytes 76
  4.5 4.4 %collective-permute-start.2 = (f32[72,128]{1,0:T(8,128)S(1)}, f32[72,128]{1,0:T(8,128)S(1)}, u32[]{:S(2)}, u32[]{:S(2)}) collective-permute-start(f32[72,128]{1,0:T(8,128)S(1)} %get-tuple-element.26), channel_id=1, source_target_pairs={{0,24},{8,16},{16,8},{24,0},{1,25},{9,17},{17,9},{25,1},{2,26},{10... | collective-permute-start | bytes 110600 | tf_op jit(solution)/shard_map/ppermute | solution.py:409
  7.0 4.1 %collective-permute-start.1 = (f32[72,128]{1,0:T(8,128)S(1)}, f32[72,128]{1,0:T(8,128)S(1)}, u32[]{:S(2)}, u32[]{:S(2)}) collective-permute-start(f32[72,128]{1,0:T(8,128)S(1)} %get-tuple-element.27), channel_id=1, source_target_pairs={{0,16},{8,24},{16,0},{24,8},{1,17},{9,25},{17,1},{25,9},{2,18},{10... | collective-permute-start | bytes 110600 | tf_op jit(solution)/shard_map/ppermute | solution.py:409
  7.7 3.4 %collective-permute-start = (f32[72,128]{1,0:T(8,128)S(1)}, f32[72,128]{1,0:T(8,128)S(1)}, u32[]{:S(2)}, u32[]{:S(2)}) collective-permute-start(f32[72,128]{1,0:T(8,128)S(1)} %get-tuple-element.28), channel_id=1, source_target_pairs={{0,8},{8,0},{16,24},{24,16},{1,9},{9,1},{17,25},{25,17},{2,10},{10... | collective-permute-start | bytes 110600 | tf_op jit(solution)/shard_map/ppermute | solution.py:409
  11.1 1.0 %copy-start.1 = (f32[16,64,128]{2,1,0:T(8,128)S(1)}, f32[16,64,128]{2,1,0:T(8,128)}, u32[]{:S(2)}) copy-start(f32[16,64,128]{2,1,0:T(8,128)} %param.10) | copy-start | bytes 1572868
  13.4 6.1 %collective-permute-start.3 = (f32[128,128]{1,0:T(8,128)S(1)}, f32[128,128]{1,0:T(8,128)S(1)}, u32[]{:S(2)}, u32[]{:S(2)}) collective-permute-start(f32[128,128]{1,0:T(8,128)S(1)} %get-tuple-element.17), channel_id=1, source_target_pairs={{0,8},{8,0},{16,24},{24,16},{1,9},{9,1},{17,25},{25,17},{2,10},{10... | collective-permute-start | bytes 196616 | tf_op jit(solution)/shard_map/ppermute | solution.py:429
  13.5 6.0 %collective-permute-start.4 = (f32[128,128]{1,0:T(8,128)S(1)}, f32[128,128]{1,0:T(8,128)S(1)}, u32[]{:S(2)}, u32[]{:S(2)}) collective-permute-start(f32[128,128]{1,0:T(8,128)S(1)} %get-tuple-element.18), channel_id=1, source_target_pairs={{8,16},{16,8},{9,17},{17,9},{10,18},{18,10},{11,19},{19,11},{12,20... | collective-permute-start | bytes 196616 | tf_op jit(solution)/shard_map/ppermute | solution.py:429
  14.2 5.3 %collective-permute-start.7 = (f32[64,128]{1,0:T(8,128)S(1)}, f32[64,128]{1,0:T(8,128)S(1)}, u32[]{:S(2)}, u32[]{:S(2)}) collective-permute-start(f32[64,128]{1,0:T(8,128)S(1)} %get-tuple-element.16.refs_3_), channel_id=1, source_target_pairs={{0,1},{1,0},{2,3},{3,2},{4,5},{5,4},{6,7},{7,6},{8,9},{9,8},{10,11... | collective-permute-start | bytes 98312 | tf_op jit(solution)/shard_map/ppermute | solution.py:431
  15.7 3.7 %collective-permute-start.5 = (f32[32,128]{1,0:T(8,128)S(1)}, f32[32,128]{1,0:T(8,128)S(1)}, u32[]{:S(2)}, u32[]{:S(2)}) collective-permute-start(f32[32,128]{1,0:T(8,128)S(1)} %get-tuple-element.19), channel_id=1, source_target_pairs={{0,2},{2,0},{4,6},{6,4},{1,3},{3,1},{5,7},{7,5},{8,10},{10,8},{12,... | collective-permute-start | bytes 49160 | tf_op jit(solution)/shard_map/ppermute | solution.py:429
  17.3 2.2 %collective-permute-start.6 = (f32[32,128]{1,0:T(8,128)S(1)}, f32[32,128]{1,0:T(8,128)S(1)}, u32[]{:S(2)}, u32[]{:S(2)}) collective-permute-start(f32[32,128]{1,0:T(8,128)S(1)} %get-tuple-element.20), channel_id=1, source_target_pairs={{2,4},{4,2},{3,5},{5,3},{10,12},{12,10},{11,13},{13,11},{18,20},{2... | collective-permute-start | bytes 49160 | tf_op jit(solution)/shard_map/ppermute | solution.py:429
